TPU v7x, 32 devices: a whole 2x2x4 slice. The times are simulated.
32 devices in a mesh: dp: 2 (over x), tp: 4 (over z), ep: 4 (over y, core).
Axes of the slice: x: 2, y: 2, z: 4, core: 2. Of those that a mesh axis runs over, the one named last changes fastest.
Arguments:
- hidden_in: bfloat16 [96, 256, 2048], P(('dp', 'ep'), 'tp'), parts along dimension 0
- ln_attn: float32 [2, 2048], replicated
- ln_ffn: float32 [2, 2048], replicated
- w_query: bfloat16 [2, 2048, 2048], P(None, None, 'tp')
- w_key: bfloat16 [2, 2048, 2048], P(None, None, 'tp')
- w_value: bfloat16 [2, 2048, 2048], P(None, None, 'tp')
- w_out: bfloat16 [2, 2048, 2048], P(None, 'tp')
- bias_table: float32 [2, 16, 32], P(None, 'tp')
- w_gate: bfloat16 [2048, 1024], P(None, 'tp')
- w_up: bfloat16 [2048, 1024], P(None, 'tp')
- w_down: bfloat16 [1024, 2048], P('tp')
- w_router: float32 [2048, 64], replicated
- expert_in: bfloat16 [64, 2048, 1024], P(('tp', 'ep'))
- expert_out: bfloat16 [64, 1024, 2048], P(('tp', 'ep'))
- expert_ids: int32 [96, 256, 2], P(('dp', 'ep'), 'tp'), parts along dimension 0
Outputs:
- output 1: bfloat16 [96, 256, 2048], P(('dp', 'ep'), 'tp'), parts along dimension 0
- output 2: bfloat16 [2, 96, 16, 256, 128], P(None, ('dp', 'ep'), 'tp'), parts along dimension 1
- output 3: bfloat16 [2, 96, 16, 256, 128], P(None, ('dp', 'ep'), 'tp'), parts along dimension 1
There are 2 independent parts. A program takes and returns all parts, laid end to end along the dimension named above; an argument that names none is the same for every part.
All inputs are finite; a program needn't handle non-finite values.
Results may differ from a plain program's by a relative error of at most 0.0146216.
Values are sent between devices in bfloat16 or wider.
A program may use at most 1 GiB of HBM per device.

v0:
```python
import jax
import jax.numpy as jnp
from jax import lax
from jax.sharding import PartitionSpec as P

EXACT_BUCKETS = 16
THRESHOLDS = (18, 20, 23, 26, 30, 34, 39, 45, 51, 58, 66, 76, 86, 98, 112)
EPSILON = 1e-6


def bucket_of(rel_pos):
    bucket_idx = jnp.minimum(rel_pos, EXACT_BUCKETS)
    for threshold in THRESHOLDS:
        bucket_idx = bucket_idx + (rel_pos >= threshold).astype(jnp.int32)
    return bucket_idx


def rms_norm(rows_in, ln_scale):
    wide_rows = rows_in.astype(jnp.float32)
    inv_rms = lax.rsqrt(jnp.mean(wide_rows * wide_rows, axis=-1, keepdims=True) + EPSILON)
    return (wide_rows * inv_rms * ln_scale).astype(jnp.bfloat16)


def causal_bias(bias_rows, seq_len):
    positions = jnp.arange(seq_len)
    rel_pos = positions[:, None] - positions[None, :]
    bias_full = jnp.take(bias_rows, bucket_of(jnp.maximum(rel_pos, 0)), axis=1)
    return jnp.where(rel_pos[None] >= 0, bias_full, -jnp.inf)


def attend(normed_full, w_query, w_key, w_value, bias_rows):
    local_batch, seq_len, d_model = normed_full.shape
    num_heads = bias_rows.shape[0]
    head_dim = w_query.shape[1] // num_heads

    def project(weight):
        projected = jnp.einsum('btd,dk->btk', normed_full, weight, preferred_element_type=jnp.float32)
        return projected.astype(jnp.bfloat16).reshape(local_batch, seq_len, num_heads, head_dim)

    queries = project(w_query)
    keys_full = project(w_key)
    values_full = project(w_value)
    scores = jnp.einsum('bqhd,bkhd->bhqk', queries, keys_full, preferred_element_type=jnp.float32)
    scores = scores * (head_dim ** -0.5) + causal_bias(bias_rows, seq_len)[None]
    attn_probs = jax.nn.softmax(scores, axis=-1).astype(jnp.bfloat16)
    context = jnp.einsum('bhqk,bkhd->bqhd', attn_probs, values_full, preferred_element_type=jnp.float32)
    context = context.astype(jnp.bfloat16).reshape(local_batch, seq_len, num_heads * head_dim)
    return context, jnp.swapaxes(keys_full, 1, 2), jnp.swapaxes(values_full, 1, 2)


def attention_block(hidden, ln_scale, w_query, w_key, w_value, w_out, bias_rows):
    normed = rms_norm(hidden, ln_scale)
    gathered = lax.all_gather(normed, 'tp', axis=1, tiled=True)
    context, keys_cache, values_cache = attend(gathered, w_query, w_key, w_value, bias_rows)
    part_sum = jnp.einsum('crl,le->cre', context, w_out, preferred_element_type=jnp.float32)
    reduced = lax.psum_scatter(part_sum, 'tp', scatter_dimension=1, tiled=True)
    return (hidden.astype(jnp.float32) + reduced).astype(jnp.bfloat16), keys_cache, values_cache


def ffn_block(hidden, ln_scale, w_gate, w_up, w_down):
    normed = rms_norm(hidden, ln_scale)
    gathered = lax.all_gather(normed, 'tp', axis=1, tiled=True)
    gate_pre = jnp.einsum('btd,df->btf', gathered, w_gate, preferred_element_type=jnp.float32)
    up_pre = jnp.einsum('btd,df->btf', gathered, w_up, preferred_element_type=jnp.float32)
    ffn_hidden = (jax.nn.gelu(gate_pre) * up_pre).astype(jnp.bfloat16)
    part_sum = jnp.einsum('btf,fd->btd', ffn_hidden, w_down, preferred_element_type=jnp.float32)
    reduced = lax.psum_scatter(part_sum, 'tp', scatter_dimension=1, tiled=True)
    return (hidden.astype(jnp.float32) + reduced).astype(jnp.bfloat16)


def slot_table(choices, num_experts):
    experts = jnp.arange(num_experts, dtype=jnp.int32)
    first_hot = (choices[..., 0:1] == experts).astype(jnp.int32)
    second_hot = (choices[..., 1:2] == experts).astype(jnp.int32)
    first_pos = jnp.sum((jnp.cumsum(first_hot, axis=-2) - 1) * first_hot, axis=-1)
    second_base = jnp.cumsum(second_hot, axis=-2) - 1 + jnp.sum(first_hot, axis=-2, keepdims=True)
    second_pos = jnp.sum(second_base * second_hot, axis=-1)
    return jnp.stack([first_pos, second_pos], axis=-1)


def route(normed, choices, w_router, num_experts, capacity):
    logits = jnp.dot(normed.astype(jnp.float32), w_router, precision=lax.Precision.HIGHEST)
    router_probs = jax.nn.softmax(logits, axis=-1)
    picked = jnp.take_along_axis(router_probs, choices, axis=-1)
    gate_weights = picked / jnp.sum(picked, axis=-1, keepdims=True)
    position = slot_table(choices, num_experts)
    slot_ids = jnp.where(position < capacity, choices * capacity + position, -1)
    columns = jnp.arange(num_experts * capacity, dtype=jnp.int32)
    select = (slot_ids[:, :, None] == columns).astype(jnp.bfloat16)
    return gate_weights, select


def moe_block(hidden, ln_scale, w_router, expert_in, expert_out, expert_ids):
    local_batch, local_seq, d_model = hidden.shape
    tokens = local_batch * local_seq
    num_experts = w_router.shape[1]
    local_experts = expert_in.shape[0]
    groups = num_experts // local_experts
    capacity = 4 * tokens // num_experts
    normed = rms_norm(hidden, ln_scale).reshape(tokens, d_model)
    gate_weights, select = route(normed, expert_ids.reshape(tokens, 2), w_router, num_experts, capacity)
    dispatched = jnp.einsum('ncs,nd->sd', select, normed, preferred_element_type=jnp.float32).astype(jnp.bfloat16)
    dispatched = dispatched.reshape(groups, local_experts, capacity, d_model)
    received = lax.all_to_all(dispatched, ('tp', 'ep'), 0, 2, tiled=True)
    expert_rows = received.reshape(local_experts, groups * capacity, d_model)
    expert_hidden = jnp.einsum('erd,edf->erf', expert_rows, expert_in, preferred_element_type=jnp.float32)
    expert_hidden = jax.nn.gelu(expert_hidden).astype(jnp.bfloat16)
    expert_result = jnp.einsum('erf,efd->erd', expert_hidden, expert_out, preferred_element_type=jnp.float32).astype(jnp.bfloat16)
    expert_result = expert_result.reshape(1, local_experts, groups * capacity, d_model)
    returned = lax.all_to_all(expert_result, ('tp', 'ep'), 2, 0, tiled=True)
    returned = returned.reshape(num_experts * capacity, d_model)
    gathered_out = jnp.einsum('ncs,sd->ncd', select, returned, preferred_element_type=jnp.float32)
    moe_sum = jnp.sum(gate_weights[:, :, None] * gathered_out, axis=1).reshape(local_batch, local_seq, d_model)
    return (hidden.astype(jnp.float32) + moe_sum).astype(jnp.bfloat16)


def solution(mesh):
    act_spec = P(('dp', 'ep'), 'tp', None)
    col_spec = P(None, None, 'tp')
    row_spec = P(None, 'tp', None)
    expert_spec = P(('tp', 'ep'), None, None)
    cache_spec = P(None, ('dp', 'ep'), 'tp', None, None)
    in_specs = (act_spec, P(), P(), col_spec, col_spec, col_spec, row_spec, row_spec,
                P(None, 'tp'), P(None, 'tp'), P('tp', None), P(), expert_spec, expert_spec, act_spec)

    def device_fn(hidden_in, ln_attn, ln_ffn, w_query, w_key, w_value, w_out, bias_table, w_gate, w_up, w_down, w_router, expert_in, expert_out, expert_ids):
        hidden, keys_zero, values_zero = attention_block(hidden_in, ln_attn[0], w_query[0], w_key[0], w_value[0], w_out[0], bias_table[0])
        hidden = ffn_block(hidden, ln_ffn[0], w_gate, w_up, w_down)
        hidden, keys_one, values_one = attention_block(hidden, ln_attn[1], w_query[1], w_key[1], w_value[1], w_out[1], bias_table[1])
        hidden = moe_block(hidden, ln_ffn[1], w_router, expert_in, expert_out, expert_ids)
        return hidden, jnp.stack([keys_zero, keys_one]), jnp.stack([values_zero, values_one])

    return jax.shard_map(device_fn, mesh=mesh, in_specs=in_specs, out_specs=(act_spec, cache_spec, cache_spec), check_vma=False)
```

profile of v0, /device:TPU:13, one launch (start us, length us, event | category | flops | bytes accessed | tf_op | source)
XLA Modules:
  0.0 3021.1 jit_solution(4871060953361889279)
XLA Ops:
  17.1 215.5 %gather_fusion.2 = f32[65536,4]{1,0:T(8,128)} fusion(f32[4,32]{0,1:T(8,128)S(1)} %copy.119, s32[65536]{0:T(1024)S(1)} %broadcast_clamp_fusion), kind=kCustom, calls=%fused_computation.1.clone | custom fusion | bytes 2359296 | tf_op jit(solution)/shard_map/jit(_take)/gather | solution.py:27
  232.6 19.0 copy.120
  251.6 215.5 %gather_fusion.1 = f32[65536,4]{1,0:T(8,128)} fusion(f32[4,32]{0,1:T(8,128)S(1)} %copy.111, s32[65536]{0:T(1024)S(1)} %broadcast_clamp_fusion), kind=kCustom, calls=%fused_computation.clone | custom fusion | bytes 2359296 | tf_op jit(solution)/shard_map/jit(_take)/gather | solution.py:27
  467.1 19.8 copy.112
  489.4 10.5 convert_bitcast_fusion.4
  499.9 7.1 convert_bitcast_fusion.5
  508.7 6.2 fusion.146
  515.0 13.4 convert_bitcast_fusion.6
  533.3 13.9 fusion.76
  548.0 414.1 %reduce-scatter.4.cloned.1.call-done = f32[12,64,2048]{2,1,0:T(8,128)} async-done(((f32[12,256,2048]{2,1,0:T(8,128)}), f32[12,64,2048]{2,1,0:T(8,128)}) %reduce-scatter.4.cloned.1.call-update) | async-done | bytes 6291472 | tf_op jit(solution)/shard_map/reduce_scatter | solution.py:56
  971.4 216.6 %all-gather.6.cloned.1.call-done = bf16[12,256,2048]{2,1,0:T(8,128)(2,1)} async-done(((bf16[12,64,2048]{2,1,0:T(8,128)(2,1)}), bf16[12,256,2048]{2,1,0:T(8,128)(2,1)}) %all-gather.6.cloned.1.call-update) | async-done | bytes 12582928 | tf_op jit(solution)/shard_map/all_gather | solution.py:62
  1188.0 9.9 fusion.97
  1197.9 20.8 fusion.89
  1218.8 415.0 %reduce-scatter.6.cloned.1.call-done = f32[12,64,2048]{2,1,0:T(8,128)} async-done(((f32[12,256,2048]{2,1,0:T(8,128)}), f32[12,64,2048]{2,1,0:T(8,128)}) %reduce-scatter.6.cloned.1.call-update) | async-done | bytes 6291472 | tf_op jit(solution)/shard_map/reduce_scatter | solution.py:67
  1642.8 217.0 %all-gather.8.cloned.1.call-done = bf16[12,256,2048]{2,1,0:T(8,128)(2,1)} async-done(((bf16[12,64,2048]{2,1,0:T(8,128)(2,1)}), bf16[12,256,2048]{2,1,0:T(8,128)(2,1)}) %all-gather.8.cloned.1.call-update) | async-done | bytes 12582928 | tf_op jit(solution)/shard_map/all_gather | solution.py:53
  1859.8 10.6 convert_bitcast_fusion.1
  1870.5 7.0 convert_bitcast_fusion.2
  1879.3 6.1 fusion.147
  1885.5 13.5 convert_bitcast_fusion.3
  1904.0 13.9 fusion.71
  1923.4 7.4 convert_reduce_fusion
  1930.8 402.2 %reduce-scatter.8.cloned.1.call-done = f32[12,64,2048]{2,1,0:T(8,128)} async-done(((f32[12,256,2048]{2,1,0:T(8,128)}), f32[12,64,2048]{2,1,0:T(8,128)}) %reduce-scatter.8.cloned.1.call-update) | async-done | bytes 6291472 | tf_op jit(solution)/shard_map/reduce_scatter | solution.py:56
  2341.2 10.8 fusion.150
  2352.1 279.2 %all_to_all.30 = bf16[16,4,48,2048]{3,2,1,0:T(8,128)(2,1)S(1)} all-to-all(bf16[16,4,48,2048]{3,2,1,0:T(8,128)(2,1)S(1)} %bitcast.210), channel_id=1, replica_groups=mesh['dp'=2,'tp'=4,'ep'=4] {'tp','ep'}, dimensions={0} | all-to-all | bytes 25165824 | tf_op jit(solution)/shard_map/all_to_all | solution.py:104
  2633.2 19.4 fusion.149
  2652.6 24.5 convert_bitcast_fusion
  2677.1 17.1 copy.132
  2715.8 12.7 gather_fusion
  2729.7 242.3 %all-to-all-done.1 = bf16[1,4,768,2048]{3,1,0,2:T(4,128)(2,1)} async-done(((bf16[1,4,768,2048]{3,1,0,2:T(4,128)(2,1)}), bf16[1,4,768,2048]{3,1,0,2:T(4,128)(2,1)}, u32[]{:S(2)}, u32[]{:S(2)}) %all-to-all-start.1) | async-done | bytes 12582944 | tf_op jit(solution)/shard_map/all_to_all | solution.py:110
  2972.0 11.7 copy.133
  2983.8 24.3 multiply_reduce_fusion
  3008.0 5.8 fusion.30
  (141 shorter events, 83.0 us)
Async XLA Ops:
  7.2 1190.7 %copy-start = (bf16[256,2048]{1,0:T(8,128)(2,1)S(1)}, bf16[256,2048]{1,0:T(8,128)(2,1)}, u32[]{:S(2)}) copy-start(bf16[256,2048]{1,0:T(8,128)(2,1)} %param.27) | copy-start | bytes 3145732
  7.2 8.5 copy-start.26
  7.2 482.2 %all-gather.4.cloned.1.call-start = ((), (), s32[]{:S(2)}) async-start(), calls=%async_computation.5 | async-start | bytes 15728640 | tf_op jit(solution)/shard_map/all_gather | solution.py:53
  15.7 946.4 %reduce-scatter.4.cloned.1.call-start = ((), (), s32[]{:S(2)}) async-start(), calls=%async_computation.6 | async-start | bytes 31457280 | tf_op jit(solution)/shard_map/reduce_scatter | solution.py:56
  489.3 10.5 copy-start.27
  489.3 10.5 copy-start.29
  499.9 7.1 copy-start.6
  514.9 13.4 copy-start.9
  547.2 640.7 %all-gather.6.cloned.1.call-start = ((), (), s32[]{:S(2)}) async-start(), calls=%async_computation.7 | async-start | bytes 15728640 | tf_op jit(solution)/shard_map/all_gather | solution.py:62
  970.9 227.0 %copy-start.16 = (bf16[2048,256]{1,0:T(8,128)(2,1)S(1)}, bf16[2048,256]{1,0:T(8,128)(2,1)}, u32[]{:S(2)}) copy-start(bf16[2048,256]{1,0:T(8,128)(2,1)} %param.26) | copy-start | bytes 3145732
  970.9 662.9 %reduce-scatter.6.cloned.1.call-start = ((), (), s32[]{:S(2)}) async-start(), calls=%async_computation.8 | async-start | bytes 31457280 | tf_op jit(solution)/shard_map/reduce_scatter | solution.py:67
  1218.8 421.5 %copy-start.22 = (f32[1,2048]{1,0:T(1,128)S(1)}, f32[1,2048]{1,0:T(1,128)}, u32[]{:S(2)}) copy-start(f32[1,2048]{1,0:T(1,128)} %get-tuple-element.18) | copy-start | bytes 24580
  1218.8 641.0 %all-gather.8.cloned.1.call-start = ((), (), s32[]{:S(2)}) async-start(), calls=%async_computation.9 | async-start | bytes 15728640 | tf_op jit(solution)/shard_map/all_gather | solution.py:53
  1642.7 690.3 %reduce-scatter.8.cloned.1.call-start = ((), (), s32[]{:S(2)}) async-start(), calls=%async_computation.10 | async-start | bytes 31457280 | tf_op jit(solution)/shard_map/reduce_scatter | solution.py:56
  1859.8 10.6 copy-start.28
  1859.8 10.7 copy-start.30
  1870.4 7.0 copy-start.7
  1885.4 13.5 copy-start.10
  1918.7 419.0 %copy-start.18 = (s32[768,2]{0,1:T(2,128)}, s32[768,2]{0,1:T(2,128)S(1)}, u32[]{:S(2)}) copy-start(s32[768,2]{0,1:T(2,128)S(1)} %reshape.270) | copy-start | bytes 18436
  1923.4 414.3 %copy-start.23 = (s32[768,2]{0,1:T(2,128)}, s32[768,2]{0,1:T(2,128)S(1)}, u32[]{:S(2)}) copy-start(s32[768,2]{0,1:T(2,128)S(1)} %compare_select_fusion.4) | copy-start | bytes 18436
  2337.7 3.5 copy-start.13
  2340.3 11.8 copy-start.11
  2694.2 277.8 %all-to-all-start.1 = ((bf16[1,4,768,2048]{3,1,0,2:T(4,128)(2,1)}), bf16[1,4,768,2048]{3,1,0,2:T(4,128)(2,1)}, u32[]{:S(2)}, u32[]{:S(2)}) async-start(bf16[1,4,768,2048]{3,1,0,2:T(4,128)(2,1)} %copy.132), calls=%async_computation.4 | async-start | bytes 25165824 | tf_op jit(solution)/shard_map/all_to_all | solution.py:110
  2700.1 5.8 copy-start.15
  2703.0 3.7 copy-start.8
  2707.5 5.2 copy-start.12
  2707.5 5.2 copy-start.17
  2715.7 13.6 copy-start.21
  2715.8 13.9 copy-start.19
  2972.0 11.8 copy-start.24
  2983.7 24.3 copy-start.4
  3008.0 5.8 copy-start.1
  (6 other events, 8.4 us)
Sparse Core Ops, SparseCore 0:
  15.8 216.6 all-gather.3
  547.4 414.6 reduce-scatter.3
  971.1 216.8 all-gather.5
  1218.9 414.9 reduce-scatter.5
  1642.9 216.8 all-gather.7
  1918.1 414.9 reduce-scatter.7
where the time goes:
time: 3030 us; the launch traced here: 3020 us
  waiting for transfers between devices  1910 us (63%)
  local copies, waits for them, and re-layouts  532 us (18%)
  blocking collectives  279 us (9%)
  matrix products  216 us (7%)
  other arithmetic  64.7 us (2%)
    reduce_scatter x2, waiting for transfers between devices, attention_block(): reduced = lax.psum_scatter(part_sum, 'tp', scatter_dimension=1, tiled=True)  816 us
    gather x4, local copies, waits for them, and re-layouts, causal_bias(): bias_full = jnp.take(bias_rows, bucket_of(jnp.maximum(rel_pos, 0)), axis=1)  470 us
    reduce_scatter x1, waiting for transfers between devices, ffn_block(): reduced = lax.psum_scatter(part_sum, 'tp', scatter_dimension=1, tiled=True)  415 us
    all_to_all x1, blocking collectives, moe_block(): received = lax.all_to_all(dispatched, ('tp', 'ep'), 0, 2, tiled=True)  279 us
    all_to_all x1, waiting for transfers between devices, moe_block(): returned = lax.all_to_all(expert_result, ('tp', 'ep'), 2, 0, tiled=True)  242 us
    all_gather x2, waiting for transfers between devices, attention_block(): gathered = lax.all_gather(normed, 'tp', axis=1, tiled=True)  217 us
    all_gather x1, waiting for transfers between devices, ffn_block(): gathered = lax.all_gather(normed, 'tp', axis=1, tiled=True)  217 us
    dot_general x6, matrix products, project(): jnp.einsum('btd,dk->btk', normed_full, weight, preferred_element_type=jnp...  62.1 us
  transfers between devices with their start and end apart: 7, of which 6 were waited for; matrix products, arithmetic and copies ran while one was open for 17% of the time, Pallas kernels for 0%

commit v1 on v0

v1 whole, which is shorter than its diff:
```python
import jax
import jax.numpy as jnp
from jax import lax
from jax.sharding import PartitionSpec as P

EXACT_BUCKETS = 16
THRESHOLDS = (18, 20, 23, 26, 30, 34, 39, 45, 51, 58, 66, 76, 86, 98, 112)
EPSILON = 1e-6


def bucket_of(rel_pos):
    bucket_idx = jnp.minimum(rel_pos, EXACT_BUCKETS)
    for threshold in THRESHOLDS:
        bucket_idx = bucket_idx + (rel_pos >= threshold).astype(jnp.int32)
    return bucket_idx


def rms_norm(rows_in, ln_scale):
    wide_rows = rows_in.astype(jnp.float32)
    inv_rms = lax.rsqrt(jnp.mean(wide_rows * wide_rows, axis=-1, keepdims=True) + EPSILON)
    return (wide_rows * inv_rms * ln_scale).astype(jnp.bfloat16)


def causal_bias(bias_rows, seq_len):
    positions = jnp.arange(seq_len)
    rel_pos = (positions[:, None] - positions[None, :])[None]
    starts = tuple(range(EXACT_BUCKETS + 1)) + THRESHOLDS
    bias_full = jnp.broadcast_to(bias_rows[:, 0][:, None, None], (bias_rows.shape[0], seq_len, seq_len))
    for bucket, start in enumerate(starts[1:], 1):
        bias_full = jnp.where(rel_pos >= start, bias_rows[:, bucket][:, None, None], bias_full)
    return jnp.where(rel_pos >= 0, bias_full, -jnp.inf)


def attend(normed_full, w_query, w_key, w_value, bias_full):
    local_batch, seq_len, d_model = normed_full.shape
    num_heads = bias_full.shape[0]
    head_dim = w_query.shape[1] // num_heads

    def project(weight):
        projected = jnp.einsum('btd,dk->btk', normed_full, weight, preferred_element_type=jnp.float32)
        return projected.astype(jnp.bfloat16).reshape(local_batch, seq_len, num_heads, head_dim)

    queries = project(w_query)
    keys_full = project(w_key)
    values_full = project(w_value)
    scores = jnp.einsum('bqhd,bkhd->bhqk', queries, keys_full, preferred_element_type=jnp.float32)
    scores = scores * (head_dim ** -0.5) + bias_full[None]
    attn_probs = jax.nn.softmax(scores, axis=-1).astype(jnp.bfloat16)
    context = jnp.einsum('bhqk,bkhd->bqhd', attn_probs, values_full, preferred_element_type=jnp.float32)
    context = context.astype(jnp.bfloat16).reshape(local_batch, seq_len, num_heads * head_dim)
    return context, jnp.swapaxes(keys_full, 1, 2), jnp.swapaxes(values_full, 1, 2)


def after(values, anchor):
    return lax.optimization_barrier((values, anchor))


def gather_weight(piece):
    return lax.all_gather(piece, ('tp', 'dp', 'ep'), axis=0, tiled=True)


def shard_piece(local, parts, index):
    rows = local.shape[0] // parts
    return lax.dynamic_slice_in_dim(local, index * rows, rows, axis=0)


def add_rows(hidden, lhs, weight):
    product = jnp.einsum('btf,fd->btd', lhs, weight, preferred_element_type=jnp.float32)
    return (hidden.astype(jnp.float32) + product).astype(jnp.bfloat16)


def ffn_rows(hidden, ln_scale, w_gate, w_up, w_down):
    normed = rms_norm(hidden, ln_scale)
    gate_pre = jnp.einsum('btd,fd->btf', normed, w_gate, preferred_element_type=jnp.float32)
    up_pre = jnp.einsum('btd,fd->btf', normed, w_up, preferred_element_type=jnp.float32)
    ffn_hidden = (jax.nn.gelu(gate_pre) * up_pre).astype(jnp.bfloat16)
    return add_rows(hidden, ffn_hidden, w_down)


def slot_table(choices, num_experts):
    experts = jnp.arange(num_experts, dtype=jnp.int32)
    first_hot = (choices[..., 0:1] == experts).astype(jnp.int32)
    second_hot = (choices[..., 1:2] == experts).astype(jnp.int32)
    first_pos = jnp.sum((jnp.cumsum(first_hot, axis=-2) - 1) * first_hot, axis=-1)
    second_base = jnp.cumsum(second_hot, axis=-2) - 1 + jnp.sum(first_hot, axis=-2, keepdims=True)
    second_pos = jnp.sum(second_base * second_hot, axis=-1)
    return jnp.stack([first_pos, second_pos], axis=-1)


def moe_plan(choices, num_experts, capacity):
    experts = jnp.arange(num_experts, dtype=jnp.int32)
    position = slot_table(choices, num_experts)
    hot = choices[:, :, None] == experts
    slot_ids = jnp.where(position < capacity, choices * capacity + position, -1)
    return slot_ids, hot


def moe_block(hidden, ln_scale, w_router, expert_in, expert_out, plan):
    slot_ids, hot = plan
    local_batch, local_seq, d_model = hidden.shape
    tokens = local_batch * local_seq
    num_experts = w_router.shape[1]
    local_experts = expert_in.shape[0]
    groups = num_experts // local_experts
    capacity = 4 * tokens // num_experts
    axes = ('tp', 'ep')
    normed = rms_norm(hidden, ln_scale).reshape(tokens, d_model)
    wide = normed.astype(jnp.float32)
    slot_order = jnp.arange(num_experts * capacity, dtype=jnp.int32).reshape(groups, local_experts, capacity)
    logits = jnp.dot(wide, w_router, precision=lax.Precision.HIGHEST)
    router_probs = jax.nn.softmax(logits, axis=-1)
    picked = jnp.sum(jnp.where(hot, router_probs[:, None, :], 0.0), axis=-1)
    gate_weights = picked / jnp.sum(picked, axis=-1, keepdims=True)

    returned = []
    step = local_experts // PARTS
    for part in range(PARTS):
        columns = slot_order[:, part * step:(part + 1) * step].reshape(-1)
        select = ((slot_ids[:, 0, None] == columns) | (slot_ids[:, 1, None] == columns)).astype(jnp.bfloat16)
        rows_out = jnp.einsum('ns,nd->sd', select, normed, preferred_element_type=jnp.float32).astype(jnp.bfloat16)
        received = lax.all_to_all(rows_out, axes, 0, 0, tiled=True).reshape(groups, step, capacity, d_model)
        results = []
        for item in range(step):
            expert = part * step + item
            expert_hidden = jnp.einsum('gcd,df->gcf', received[:, item], expert_in[expert], preferred_element_type=jnp.float32)
            expert_hidden = jax.nn.gelu(expert_hidden).astype(jnp.bfloat16)
            result = jnp.einsum('gcf,fd->gcd', expert_hidden, expert_out[expert], preferred_element_type=jnp.float32)
            results.append(result.astype(jnp.bfloat16))
        result = jnp.stack(results, axis=1).reshape(groups * step * capacity, d_model)
        returned.append(lax.all_to_all(result, axes, 0, 0, tiled=True))
    moe_sum = None
    for part in range(PARTS):
        columns = slot_order[:, part * step:(part + 1) * step].reshape(-1)
        rows_back = returned[part]
        if part:
            rows_back, moe_sum = after(rows_back, moe_sum)
        one_hot = (slot_ids[:, :, None] == columns).astype(jnp.bfloat16)
        chosen = jnp.einsum('ncs,sd->ncd', one_hot, rows_back, preferred_element_type=jnp.float32)
        part_sum = jnp.sum(gate_weights[:, :, None] * chosen, axis=1)
        moe_sum = part_sum if moe_sum is None else moe_sum + part_sum
    moe_sum = moe_sum.reshape(local_batch, local_seq, d_model)
    return (hidden.astype(jnp.float32) + moe_sum).astype(jnp.bfloat16)


CHUNKS = 2
PARTS = 2


def solution(mesh):
    act_spec = P(('dp', 'ep'), 'tp', None)
    col_spec = P(None, None, 'tp')
    row_spec = P(None, 'tp', None)
    expert_spec = P(('tp', 'ep'), None, None)
    cache_spec = P(None, ('dp', 'ep'), 'tp', None, None)
    in_specs = (act_spec, P(), P(), col_spec, col_spec, col_spec, row_spec, row_spec,
                P(None, 'tp'), P(None, 'tp'), P('tp', None), P(), expert_spec, expert_spec, act_spec)
    tp_size = mesh.shape['tp']
    plane = mesh.shape['dp'] * mesh.shape['ep']

    def device_fn(hidden_in, ln_attn, ln_ffn, w_query, w_key, w_value, w_out, bias_table, w_gate, w_up, w_down, w_router, expert_in, expert_out, expert_ids):
        local_batch, local_seq, d_model = hidden_in.shape
        seq_len = local_seq * tp_size
        spot = lax.axis_index(('dp', 'ep'))
        size = local_batch // CHUNKS
        tokens = local_batch * local_seq
        num_experts = w_router.shape[1]
        plan = moe_plan(expert_ids.reshape(tokens, 2), num_experts, 4 * tokens // num_experts)

        parts_zero = [shard_piece(w_out[0], plane, spot), shard_piece(w_gate.T, plane, spot),
                      shard_piece(w_up.T, plane, spot), shard_piece(w_down, plane, spot)]
        piece_zero = jnp.concatenate(parts_zero, axis=0)
        piece_one = shard_piece(w_out[1], plane, spot)
        biases = [causal_bias(bias_table[layer], seq_len) for layer in range(2)]

        def gather(rows):
            return lax.all_gather(rows, 'tp', axis=1, tiled=True)

        keys, values = [[], []], [[], []]

        def attention(layer, gathered):
            context, keys_new, values_new = attend(gathered, w_query[layer], w_key[layer], w_value[layer], biases[layer])
            keys[layer].append(keys_new)
            values[layer].append(values_new)
            context = context.reshape(size, tp_size, local_seq, context.shape[-1])
            return jnp.swapaxes(context, 0, 1)

        def project_out(rows, context, weight):
            weight = weight.reshape(tp_size, -1, d_model)
            product = jnp.einsum('sbtf,sfd->btd', context, weight, preferred_element_type=jnp.float32)
            return (rows.astype(jnp.float32) + product).astype(jnp.bfloat16)

        def attention_chain(layer, gathered):
            arrived, own = [], None
            for rows in gathered:
                if own is not None:
                    rows, own = after(rows, own)
                    arrived.append(lax.all_to_all(own, 'tp', 0, 0, tiled=True))
                own = attention(layer, rows)
                if arrived:
                    own, arrived[-1] = after(own, arrived[-1])
            arrived.append(lax.all_to_all(own, 'tp', 0, 0, tiled=True))
            return arrived

        hidden = [hidden_in[c * size:(c + 1) * size] for c in range(CHUNKS)]
        gathered = [gather(rms_norm(rows, ln_attn[0])) for rows in hidden]
        piece_zero, gathered[-1] = after(piece_zero, gathered[-1])
        joined = gather_weight(piece_zero).reshape(tp_size * plane, -1, d_model)
        weights_zero, first = [], 0
        for part in parts_zero:
            weights_zero.append(joined[:, first:first + part.shape[0]].reshape(-1, d_model))
            first += part.shape[0]
        out_zero, gate, up, down = weights_zero
        contexts = attention_chain(0, gathered)
        gathered = []
        for c in range(CHUNKS):
            rows = hidden[c]
            if c:
                rows, normed = after(rows, normed)
                gathered.append(gather(normed))
            rows = project_out(rows, contexts[c], out_zero)
            rows = ffn_rows(rows, ln_ffn[0], gate, up, down)
            hidden[c] = rows
            normed = rms_norm(rows, ln_attn[1])
        gathered.append(gather(normed))
        piece_one, gathered[0] = after(piece_one, gathered[0])
        out_one = gather_weight(piece_one)
        contexts = attention_chain(1, gathered)
        hidden = jnp.concatenate([project_out(hidden[c], contexts[c], out_one) for c in range(CHUNKS)], axis=0)
        hidden = moe_block(hidden, ln_ffn[1], w_router, expert_in, expert_out, plan)

        def cache(parts):
            return jnp.stack([jnp.concatenate(rows, axis=0) for rows in parts])

        return hidden, cache(keys), cache(values)

    return jax.shard_map(device_fn, mesh=mesh, in_specs=in_specs, out_specs=(act_spec, cache_spec, cache_spec), check_vma=False)
```

time: 3030 us -> 1470 us (0.49)
  waiting for transfers between devices: 1910 us -> 927 us
  local copies, waits for them, and re-layouts: 532 us -> 80.1 us
  blocking collectives: 279 us -> 82.8 us
  starting transfers between devices: 6 us -> 45.6 us
    reduce_scatter x3 -> x0, waiting for transfers between devices: 1230 us -> none  [the longest x2 816 us: attention_block(): reduced = lax.psum_scatter(part_sum, 'tp', scatter_dimension=1, tiled=True)]
    gather x11 -> x0, local copies, waits for them, and re-layouts: 484 us -> none  [the longest x4 470 us: causal_bias(): bias_full = jnp.take(bias_rows, bucket_of(jnp.maximum(rel_pos, 0)), axis=1)]
    all_to_all x1 -> x7, waiting for transfers between devices: 242 us -> 499 us  [the longest x2 233 us: moe_block(): lax.all_to_all(rows_out, axes, 0, 0, tiled=True)]
    all_to_all x1, blocking collectives: 279 us -> 82.8 us  [attention_chain(): arrived.append(lax.all_to_all(own, 'tp', 0, 0, tiled=True))]
    all_to_all x1 -> x7, starting transfers between devices: 5.35 us -> 45.2 us  [the longest x3 23 us: attention_chain(): arrived.append(lax.all_to_all(own, 'tp', 0, 0, tiled=True))]
    dot_general x9 -> x17, matrix products: 141 us -> 156 us  [the longest x4 51.9 us: moe_block(): jnp.einsum('gcf,fd->gcd', expert_hidden, expert_out[expert], preferred_el...]
    all_gather x3 -> x6, waiting for transfers between devices: 434 us -> 428 us  [the longest x4 336 us: gather(): return lax.all_gather(rows, 'tp', axis=1, tiled=True)]
    dot_general x6 -> x12, matrix products: 62.1 us -> 62.3 us  [project(): jnp.einsum('btd,dk->btk', normed_full, weight, preferred_element_type=jnp...]
  transfers between devices with their start and end apart: 7 -> 13, of which waited for: 6 -> 12; matrix products, arithmetic and copies ran while one was open for 17% -> 19% of each run, Pallas kernels for 0% -> 0%
where the time goes in v1:
time: 1470 us; the launch traced here: 1450 us
  waiting for transfers between devices  927 us (63%)
  matrix products  239 us (16%)
  blocking collectives  82.8 us (6%)
  local copies, waits for them, and re-layouts  80.1 us (5%)
  other arithmetic  60.5 us (4%)
  starting transfers between devices  45.6 us (3%)
  between operations  16.1 us (1%)
    all_gather x4, waiting for transfers between devices, gather(): return lax.all_gather(rows, 'tp', axis=1, tiled=True)  336 us
    all_to_all x2, waiting for transfers between devices, moe_block(): lax.all_to_all(rows_out, axes, 0, 0, tiled=True)  233 us
    all_to_all x2, waiting for transfers between devices, moe_block(): returned.append(lax.all_to_all(result, axes, 0, 0, tiled=True))  209 us
    all_gather x2, waiting for transfers between devices, gather_weight(): return lax.all_gather(piece, ('tp', 'dp', 'ep'), axis=0, tiled=True)  91.7 us
    all_to_all x1, blocking collectives, attention_chain(): arrived.append(lax.all_to_all(own, 'tp', 0, 0, tiled=True))  82.8 us
    dot_general x12, matrix products, project(): jnp.einsum('btd,dk->btk', normed_full, weight, preferred_element_type=jnp...  62.3 us
    all_to_all x3, waiting for transfers between devices, attention_chain(): arrived.append(lax.all_to_all(own, 'tp', 0, 0, tiled=True))  57.3 us
    dot_general x4, matrix products, moe_block(): jnp.einsum('gcf,fd->gcd', expert_hidden, expert_out[expert], preferred_el...  51.9 us
  transfers between devices with their start and end apart: 13, of which 12 were waited for; matrix products, arithmetic and copies ran while one was open for 19% of the time, Pallas kernels for 0%

profile of v1, /device:TPU:13, one launch (start us, length us, event | category | flops | bytes accessed | tf_op | source)
XLA Modules:
  0.0 1451.3 jit_solution(3844923391477727775)
XLA Ops:
  20.6 105.1 %all-gather.7.cloned.1.call-done = bf16[6,256,2048]{2,1,0:T(8,128)(2,1)} async-done(((bf16[6,64,2048]{2,1,0:T(8,128)(2,1)}), bf16[6,256,2048]{2,1,0:T(8,128)(2,1)}) %all-gather.7.cloned.1.call-update) | async-done | bytes 6291472 | tf_op jit(solution)/shard_map/all_gather | solution.py:176
  132.6 108.7 %all-gather.9.cloned.1.call-done = bf16[6,256,2048]{2,1,0:T(8,128)(2,1)} async-done(((bf16[6,64,2048]{2,1,0:T(8,128)(2,1)}), bf16[6,256,2048]{2,1,0:T(8,128)(2,1)}) %all-gather.9.cloned.1.call-update) | async-done | bytes 6291472 | tf_op jit(solution)/shard_map/all_gather | solution.py:176
  251.9 12.7 fusion.270
  282.2 7.6 all-to-all-start
  319.6 43.7 %all-to-all-done = bf16[4,6,64,512]{3,2,1,0:T(8,128)(2,1)} async-done(((bf16[4,6,64,512]{3,2,1,0:T(8,128)(2,1)}), bf16[4,6,64,512]{3,2,1,0:T(8,128)(2,1)}, u32[]{:S(2)}, u32[]{:S(2)}) %all-to-all-start) | async-done | bytes 1572896 | tf_op jit(solution)/shard_map/all_to_all | solution.py:197
  363.3 32.6 %all-gather.11.cloned.1.call-done = bf16[5120,2048]{1,0:T(8,128)(2,1)} async-done(((bf16[160,2048]{1,0:T(8,128)(2,1)}), bf16[5120,2048]{1,0:T(8,128)(2,1)}) %all-gather.11.cloned.1.call-update) | async-done | bytes 20971536 | tf_op jit(solution)/shard_map/all_gather | solution.py:59
  395.9 8.3 slice.445
  404.3 8.5 fusion.426
  424.8 8.6 fusion.72
  436.7 82.8 %all_to_all.62 = bf16[4,6,64,512]{3,2,1,0:T(8,128)(2,1)S(1)} all-to-all(bf16[4,6,64,512]{3,2,1,0:T(8,128)(2,1)S(1)} %copy.153), channel_id=1, replica_groups=mesh['dp'=2,'tp'=4,'ep'=4] {'tp'}, dimensions={0} | all-to-all | bytes 3145728 | tf_op jit(solution)/shard_map/all_to_all | solution.py:201
  530.8 8.6 fusion.80
  543.1 38.1 %all-gather.15.cloned.1.call-done = bf16[6,256,2048]{2,1,0:T(8,128)(2,1)} async-done(((bf16[6,64,2048]{2,1,0:T(8,128)(2,1)}), bf16[6,256,2048]{2,1,0:T(8,128)(2,1)}) %all-gather.15.cloned.1.call-update) | async-done | bytes 6291472 | tf_op jit(solution)/shard_map/all_gather | solution.py:176
  612.8 83.9 %all-gather.13.cloned.1.call-done = bf16[6,256,2048]{2,1,0:T(8,128)(2,1)} async-done(((bf16[6,64,2048]{2,1,0:T(8,128)(2,1)}), bf16[6,256,2048]{2,1,0:T(8,128)(2,1)}) %all-gather.13.cloned.1.call-update) | async-done | bytes 6291472 | tf_op jit(solution)/shard_map/all_gather | solution.py:176
  698.1 7.7 all-to-all-start.2
  730.7 13.6 all-to-all-done.2
  745.6 7.8 all-to-all-start.3
  758.0 59.1 %all-gather.17.cloned.1.call-done = bf16[2048,2048]{1,0:T(8,128)(2,1)} async-done(((bf16[64,2048]{1,0:T(8,128)(2,1)}), bf16[2048,2048]{1,0:T(8,128)(2,1)}) %all-gather.17.cloned.1.call-update) | async-done | bytes 8388624 | tf_op jit(solution)/shard_map/all_gather | solution.py:59
  817.1 7.6 fusion.75
  824.8 8.2 fusion.83
  840.3 7.5 convolution_convert_fusion
  847.8 7.5 all-to-all-start.6
  855.4 9.1 convolution_convert_fusion.1
  864.5 128.4 %all-to-all-done.6 = bf16[16,96,2048]{2,1,0:T(8,128)(2,1)} async-done(((bf16[16,96,2048]{2,1,0:T(8,128)(2,1)}), bf16[16,96,2048]{2,1,0:T(8,128)(2,1)}, u32[]{:S(2)}, u32[]{:S(2)}) %all-to-all-start.6) | async-done | bytes 6291488 | tf_op jit(solution)/shard_map/all_to_all | solution.py:121
  998.0 13.0 fusion.132
  1011.0 13.0 fusion.129
  1030.8 104.4 %all-to-all-done.4 = bf16[16,96,2048]{2,1,0:T(8,128)(2,1)} async-done(((bf16[16,96,2048]{2,1,0:T(8,128)(2,1)}), bf16[16,96,2048]{2,1,0:T(8,128)(2,1)}, u32[]{:S(2)}, u32[]{:S(2)}) %all-to-all-start.4) | async-done | bytes 6291488 | tf_op jit(solution)/shard_map/all_to_all | solution.py:121
  1140.0 13.0 fusion.138
  1153.0 13.0 fusion.135
  1172.8 104.9 %all-to-all-done.7 = bf16[16,96,2048]{2,1,0:T(8,128)(2,1)} async-done(((bf16[16,96,2048]{2,1,0:T(8,128)(2,1)}), bf16[16,96,2048]{2,1,0:T(8,128)(2,1)}, u32[]{:S(2)}, u32[]{:S(2)}) %all-to-all-start.7) | async-done | bytes 6291488 | tf_op jit(solution)/shard_map/all_to_all | solution.py:130
  1300.3 16.3 %multiply_reduce_fusion.1 = f32[768,2048]{1,0:T(8,128)} fusion(f32[768,2]{0,1:T(2,128)S(1)} %broadcast_divide_fusion, bf16[1536,2048,1]{1,0,2:T(8,128)(2,1)} %bitcast.89, s32[1536]{0:T(1024)S(1)} %copy-done.57, s32[768,2]{0,1:T(2,128)S(1)} %compare_select_fusion), kind=kOutput, calls=%fused_computation.5 | convolution fusion | flops 9670754304 | bytes 12601344 | tf_op jit(solution)/shard_map/ncs,sd->ncd/dot_general | solution.py:138
  1316.6 103.7 %all-to-all-done.5 = bf16[16,96,2048]{2,1,0:T(8,128)(2,1)} async-done(((bf16[16,96,2048]{2,1,0:T(8,128)(2,1)}), bf16[16,96,2048]{2,1,0:T(8,128)(2,1)}, u32[]{:S(2)}, u32[]{:S(2)}) %all-to-all-start.5) | async-done | bytes 6291488 | tf_op jit(solution)/shard_map/all_to_all | solution.py:130
  1420.2 16.6 %multiply_reduce_fusion = f32[768,2048]{1,0:T(8,128)} fusion(f32[768,2]{0,1:T(2,128)S(1)} %broadcast_divide_fusion, bf16[1536,2048]{1,0:T(8,128)(2,1)} %bitcast.72, s32[1536]{0:T(1024)S(1)} %eq.169, s32[768,2]{0,1:T(2,128)S(1)} %compare_select_fusion), kind=kOutput, calls=%fused_computation.4 | convolution fusion | flops 9670754304 | bytes 12601344 | tf_op jit(solution)/shard_map/ncs,sd->ncd/dot_general | solution.py:138
  (308 shorter events, 231.7 us)
Async XLA Ops:
  7.2 8.4 copy-start
  7.2 118.5 %all-gather.7.cloned.1.call-start = ((), (), s32[]{:S(2)}) async-start(), calls=%async_computation.8 | async-start | bytes 7864320 | tf_op jit(solution)/shard_map/all_gather | solution.py:176
  12.6 228.7 %all-gather.9.cloned.1.call-start = ((), (), s32[]{:S(2)}) async-start(), calls=%async_computation.9 | async-start | bytes 7864320 | tf_op jit(solution)/shard_map/all_gather | solution.py:176
  13.3 382.6 %all-gather.11.cloned.1.call-start = ((), (), s32[]{:S(2)}) async-start(), calls=%async_computation.10 | async-start | bytes 21626880 | tf_op jit(solution)/shard_map/all_gather | solution.py:59
  19.7 106.1 %copy-start.59 = (f32[2,4,32]{2,1,0:T(4,128)S(1)}, f32[2,4,32]{2,1,0:T(4,128)}, u32[]{:S(2)}) copy-start(f32[2,4,32]{2,1,0:T(4,128)} %param.22) | copy-start | bytes 3076
  20.6 107.1 %copy-start.55 = (f32[2,2048]{1,0:T(2,128)S(1)}, f32[2,2048]{1,0:T(2,128)}, u32[]{:S(2)}) copy-start(f32[2,2048]{1,0:T(2,128)} %param.17) | copy-start | bytes 49156
  282.2 81.1 %all-to-all-start = ((bf16[4,6,64,512]{3,2,1,0:T(8,128)(2,1)}), bf16[4,6,64,512]{3,2,1,0:T(8,128)(2,1)}, u32[]{:S(2)}, u32[]{:S(2)}) async-start(bf16[4,6,64,512]{3,2,1,0:T(8,128)(2,1)} %copy.152), calls=%async_computation | async-start | bytes 3145728 | tf_op jit(solution)/shard_map/all_to_all | solution.py:197
  289.8 291.4 %all-gather.15.cloned.1.call-start = ((), (), s32[]{:S(2)}) async-start(), calls=%async_computation.12 | async-start | bytes 7864320 | tf_op jit(solution)/shard_map/all_gather | solution.py:176
  404.3 8.5 copy-start.3
  404.3 12.4 copy-start.10
  412.7 9.0 copy-start.20
  435.0 84.5 %slice-start = ((bf16[12,64,2048]{2,1,0:T(8,128)(2,1)}), bf16[6,64,2048]{2,1,0:T(8,128)(2,1)S(1)}, s32[]{:S(2)}) async-start(bf16[12,64,2048]{2,1,0:T(8,128)(2,1)} %param.15), calls=%async_computation.14 | async-start | bytes 3145728 | tf_op jit(solution)/shard_map/slice | solution.py:204
  435.1 261.7 %all-gather.13.cloned.1.call-start = ((), (), s32[]{:S(2)}) async-start(), calls=%async_computation.11 | async-start | bytes 7864320 | tf_op jit(solution)/shard_map/all_gather | solution.py:176
  519.6 8.3 copy-start.21
  539.4 49.3 %copy-start.27 = (bf16[6,64,2048]{2,1,0:T(8,128)(2,1)}, bf16[6,64,2048]{2,1,0:T(8,128)(2,1)S(1)}, u32[]{:S(2)}) copy-start(bf16[6,64,2048]{2,1,0:T(8,128)(2,1)S(1)} %get-tuple-element.135) | copy-start | bytes 4718596
  539.5 41.7 %copy-start.56 = (s32[12,64,2]{1,2,0:T(2,128)S(1)}, s32[12,64,2]{1,2,0:T(2,128)}, u32[]{:S(2)}) copy-start(s32[12,64,2]{1,2,0:T(2,128)} %param.29) | copy-start | bytes 18436
  541.1 276.0 %all-gather.17.cloned.1.call-start = ((), (), s32[]{:S(2)}) async-start(), calls=%async_computation.13 | async-start | bytes 8650752 | tf_op jit(solution)/shard_map/all_gather | solution.py:59
  583.5 12.3 slice-start.3
  588.8 7.0 slice-start.4
  588.8 7.0 copy-start.63
  698.1 14.7 %slice-start.5 = ((s8[6291456]{0:T(1024)(128)(4,1)}), s8[2097152]{0:T(1024)(128)(4,1)S(1)}, s32[]{:S(2)}) async-start(s8[6291456]{0:T(1024)(128)(4,1)} %bitcast.502), calls=%async_computation.19 | async-start | bytes 4194304
  698.1 46.3 %all-to-all-start.2 = ((bf16[4,6,64,512]{3,2,1,0:T(8,128)(2,1)}), bf16[4,6,64,512]{3,2,1,0:T(8,128)(2,1)}, u32[]{:S(2)}, u32[]{:S(2)}) async-start(bf16[4,6,64,512]{3,2,1,0:T(8,128)(2,1)} %copy.164), calls=%async_computation.2 | async-start | bytes 3145728 | tf_op jit(solution)/shard_map/all_to_all | solution.py:197
  705.7 7.0 copy-start.64
  745.6 79.2 %all-to-all-start.3 = ((bf16[4,6,64,512]{3,2,1,0:T(8,128)(2,1)}), bf16[4,6,64,512]{3,2,1,0:T(8,128)(2,1)}, u32[]{:S(2)}, u32[]{:S(2)}) async-start(bf16[4,6,64,512]{3,2,1,0:T(8,128)(2,1)} %copy.165), calls=%async_computation.3 | async-start | bytes 3145728 | tf_op jit(solution)/shard_map/all_to_all | solution.py:201
  824.8 8.9 copy-start.4
  840.3 7.5 copy-start.8
  847.8 7.5 copy-start.52
  847.8 145.1 %all-to-all-start.6 = ((bf16[16,96,2048]{2,1,0:T(8,128)(2,1)}), bf16[16,96,2048]{2,1,0:T(8,128)(2,1)}, u32[]{:S(2)}, u32[]{:S(2)}) async-start(bf16[16,96,2048]{2,1,0:T(8,128)(2,1)} %bitcast.465), calls=%async_computation.6 | async-start | bytes 12582912 | tf_op jit(solution)/shard_map/all_to_all | solution.py:121
  992.9 142.3 %all-to-all-start.4 = ((bf16[16,96,2048]{2,1,0:T(8,128)(2,1)}), bf16[16,96,2048]{2,1,0:T(8,128)(2,1)}, u32[]{:S(2)}, u32[]{:S(2)}) async-start(bf16[16,96,2048]{2,1,0:T(8,128)(2,1)} %bitcast.464), calls=%async_computation.4 | async-start | bytes 12582912 | tf_op jit(solution)/shard_map/all_to_all | solution.py:121
  1135.3 142.4 %all-to-all-start.7 = ((bf16[16,96,2048]{2,1,0:T(8,128)(2,1)}), bf16[16,96,2048]{2,1,0:T(8,128)(2,1)}, u32[]{:S(2)}, u32[]{:S(2)}) async-start(bf16[16,96,2048]{2,1,0:T(8,128)(2,1)} %bitcast.458), calls=%async_computation.7 | async-start | bytes 12582912 | tf_op jit(solution)/shard_map/all_to_all | solution.py:130
  1277.7 142.6 %all-to-all-start.5 = ((bf16[16,96,2048]{2,1,0:T(8,128)(2,1)}), bf16[16,96,2048]{2,1,0:T(8,128)(2,1)}, u32[]{:S(2)}, u32[]{:S(2)}) async-start(bf16[16,96,2048]{2,1,0:T(8,128)(2,1)} %bitcast.457), calls=%async_computation.5 | async-start | bytes 12582912 | tf_op jit(solution)/shard_map/all_to_all | solution.py:130
  1420.2 16.6 %copy-start.19 = (f32[768,2048]{1,0:T(8,128)S(1)}, f32[768,2048]{1,0:T(8,128)}, u32[]{:S(2)}) copy-start(f32[768,2048]{1,0:T(8,128)} %multiply_reduce_fusion.1) | copy-start | bytes 18874372
  (59 other events, 146.9 us)
Sparse Core Ops, SparseCore 0:
  12.7 112.9 all-gather.6
  127.9 113.3 all-gather.8
  244.1 151.7 all-gather.10
  435.2 145.9 all-gather.14
  583.2 113.5 all-gather.12
  699.5 117.5 all-gather.16

commit v2 on v1

--- a/solution.py
+++ b/solution.py
@@ -55,8 +55,8 @@
     return lax.optimization_barrier((values, anchor))
 
 
-def gather_weight(piece):
-    return lax.all_gather(piece, ('tp', 'dp', 'ep'), axis=0, tiled=True)
+def swap_pairs(blocks, axis, pairs):
+    return blocks + [lax.ppermute(block, axis, pairs) for block in blocks]
 
 
 def shard_piece(local, parts, index):
@@ -155,7 +155,8 @@
     in_specs = (act_spec, P(), P(), col_spec, col_spec, col_spec, row_spec, row_spec,
                 P(None, 'tp'), P(None, 'tp'), P('tp', None), P(), expert_spec, expert_spec, act_spec)
     tp_size = mesh.shape['tp']
-    plane = mesh.shape['dp'] * mesh.shape['ep']
+    dp_size, ep_size = mesh.shape['dp'], mesh.shape['ep']
+    plane = dp_size * ep_size
 
     def device_fn(hidden_in, ln_attn, ln_ffn, w_query, w_key, w_value, w_out, bias_table, w_gate, w_up, w_down, w_router, expert_in, expert_out, expert_ids):
         local_batch, local_seq, d_model = hidden_in.shape
@@ -167,9 +168,9 @@
         plan = moe_plan(expert_ids.reshape(tokens, 2), num_experts, 4 * tokens // num_experts)
 
         parts_zero = [shard_piece(w_out[0], plane, spot), shard_piece(w_gate.T, plane, spot),
-                      shard_piece(w_up.T, plane, spot), shard_piece(w_down, plane, spot)]
+                      shard_piece(w_up.T, plane, spot), shard_piece(w_down, plane, spot),
+                      shard_piece(w_out[1], plane, spot)]
         piece_zero = jnp.concatenate(parts_zero, axis=0)
-        piece_one = shard_piece(w_out[1], plane, spot)
         biases = [causal_bias(bias_table[layer], seq_len) for layer in range(2)]
 
         def gather(rows):
@@ -189,42 +190,57 @@
             product = jnp.einsum('sbtf,sfd->btd', context, weight, preferred_element_type=jnp.float32)
             return (rows.astype(jnp.float32) + product).astype(jnp.bfloat16)
 
-        def attention_chain(layer, gathered):
+        def swap_heads(context):
+            return lax.all_to_all(context, 'tp', 0, 0, tiled=True)
+
+        def attention_zero(gathered):
+            context = jnp.concatenate([attention(0, rows) for rows in gathered], axis=1)
+            arrived = swap_heads(context)
+            return [arrived[:, c * size:(c + 1) * size] for c in range(CHUNKS)]
+
+        def attention_one(gathered):
             arrived, own = [], None
             for rows in gathered:
                 if own is not None:
-                    rows, own = after(rows, own)
-                    arrived.append(lax.all_to_all(own, 'tp', 0, 0, tiled=True))
-                own = attention(layer, rows)
-                if arrived:
-                    own, arrived[-1] = after(own, arrived[-1])
-            arrived.append(lax.all_to_all(own, 'tp', 0, 0, tiled=True))
+                    arrived.append(swap_heads(own))
+                    rows, arrived[-1] = after(rows, arrived[-1])
+                own = attention(1, rows)
+            arrived.append(swap_heads(own))
             return arrived
 
         hidden = [hidden_in[c * size:(c + 1) * size] for c in range(CHUNKS)]
-        gathered = [gather(rms_norm(rows, ln_attn[0])) for rows in hidden]
-        piece_zero, gathered[-1] = after(piece_zero, gathered[-1])
-        joined = gather_weight(piece_zero).reshape(tp_size * plane, -1, d_model)
+        normed = [rms_norm(rows, ln_attn[0]) for rows in hidden]
+        column = lax.all_gather(piece_zero, 'tp', axis=0)
+        normed, column = after(normed, column)
+        gathered = [gather(rows) for rows in normed]
+        blocks = swap_pairs([column], 'dp', [(i, i ^ 1) for i in range(dp_size)])
+        for bit in (2, 1):
+            blocks = swap_pairs(blocks, 'ep', [(i, i ^ bit) for i in range(ep_size)])
+        order = [(r & 1) * ep_size + (r & 2) + (r >> 2) for r in range(plane)]
+        blocks = [blocks[order.index(q)] for q in range(plane)]
         weights_zero, first = [], 0
-        for part in parts_zero:
-            weights_zero.append(joined[:, first:first + part.shape[0]].reshape(-1, d_model))
-            first += part.shape[0]
-        out_zero, gate, up, down = weights_zero
-        contexts = attention_chain(0, gathered)
+        for number, part in enumerate(parts_zero):
+            last = first + part.shape[0]
+            whole = jnp.stack([block[:, first:last] for block in blocks])
+            if number in (0, 4):
+                ranks = [lax.dynamic_index_in_dim(whole, spot ^ q, 0, keepdims=False) for q in range(plane)]
+                whole = jnp.stack(ranks, axis=1)
+            weights_zero.append(whole.reshape(-1, d_model))
+            first = last
+        out_zero, gate, up, down, out_one = weights_zero
+        contexts = attention_zero(gathered)
         gathered = []
         for c in range(CHUNKS):
             rows = hidden[c]
             if c:
-                rows, normed = after(rows, normed)
                 gathered.append(gather(normed))
+                rows, _ = after(rows, normed)
             rows = project_out(rows, contexts[c], out_zero)
             rows = ffn_rows(rows, ln_ffn[0], gate, up, down)
             hidden[c] = rows
             normed = rms_norm(rows, ln_attn[1])
         gathered.append(gather(normed))
-        piece_one, gathered[0] = after(piece_one, gathered[0])
-        out_one = gather_weight(piece_one)
-        contexts = attention_chain(1, gathered)
+        contexts = attention_one(gathered)
         hidden = jnp.concatenate([project_out(hidden[c], contexts[c], out_one) for c in range(CHUNKS)], axis=0)
         hidden = moe_block(hidden, ln_ffn[1], w_router, expert_in, expert_out, plan)
 

time: 1470 us -> 1410 us (0.959); the launches traced: 1450 us -> 1410 us
  blocking collectives: 82.8 us -> 0 us
  local copies, waits for them, and re-layouts: 80.1 us -> 147 us
  waiting for transfers between devices: 927 us -> 875 us
    all_gather x4, waiting for transfers between devices: 336 us -> 197 us  [gather(): return lax.all_gather(rows, 'tp', axis=1, tiled=True)]
    ppermute x0 -> x7, waiting for transfers between devices: none -> 130 us  [swap_pairs(): return blocks + [lax.ppermute(block, axis, pairs) for block in blocks]]
    all_to_all x1 -> x0, blocking collectives: 82.8 us -> none  [attention_chain(): arrived.append(lax.all_to_all(own, 'tp', 0, 0, tiled=True))]
    unnamed x155 -> x227, local copies, waits for them, and re-layouts: 15.6 us -> 84.4 us
    all_gather x2 -> x1, waiting for transfers between devices: 91.7 us -> 63.8 us  [device_fn(): column = lax.all_gather(piece_zero, 'tp', axis=0)]
    slice x4 -> x2, local copies, waits for them, and re-layouts: 21.1 us -> 4.32 us  [the longest x1 4.04 us: device_fn(): w_out[1]]
  transfers between devices with their start and end apart: 13 -> 19, of which waited for: 12 -> 12; matrix products, arithmetic and copies ran while one was open for 19% -> 24% of each run, Pallas kernels for 0% -> 0%
where the time goes in v2:
time: 1410 us
  waiting for transfers between devices  875 us (62%)
  matrix products  245 us (17%)
  local copies, waits for them, and re-layouts  147 us (10%)
  other arithmetic  68.8 us (5%)
  starting transfers between devices  56.6 us (4%)
  between operations  16 us (1%)
    all_to_all x2, waiting for transfers between devices, moe_block(): lax.all_to_all(rows_out, axes, 0, 0, tiled=True)  233 us
    all_to_all x2, waiting for transfers between devices, moe_block(): returned.append(lax.all_to_all(result, axes, 0, 0, tiled=True))  209 us
    all_gather x4, waiting for transfers between devices, gather(): return lax.all_gather(rows, 'tp', axis=1, tiled=True)  197 us
    ppermute x7, waiting for transfers between devices, swap_pairs(): return blocks + [lax.ppermute(block, axis, pairs) for block in blocks]  130 us
    unnamed x227, local copies, waits for them, and re-layouts  84.4 us
    dot_general x12, matrix products, project(): jnp.einsum('btd,dk->btk', normed_full, weight, preferred_element_type=jnp...  71.3 us
    all_gather x1, waiting for transfers between devices, device_fn(): column = lax.all_gather(piece_zero, 'tp', axis=0)  63.8 us
    dot_general x4, matrix products, moe_block(): jnp.einsum('gcf,fd->gcd', expert_hidden, expert_out[expert], preferred_el...  51.9 us
  transfers between devices with their start and end apart: 19, of which 12 were waited for; matrix products, arithmetic and copies ran while one was open for 24% of the time, Pallas kernels for 0%

profile of v2, /device:TPU:13, one launch (start us, length us, event | category | flops | bytes accessed | tf_op | source)
XLA Modules:
  0.0 1408.7 jit_solution(10191338574058873038)
XLA Ops:
  27.1 63.8 %all-gather.15.cloned.1.call-done = bf16[896,2048]{1,0:T(8,128)(2,1)} async-done(((bf16[224,2048]{1,0:T(8,128)(2,1)}), bf16[896,2048]{1,0:T(8,128)(2,1)}) %all-gather.15.cloned.1.call-update) | async-done | bytes 3670032 | tf_op jit(solution)/shard_map/all_gather | solution.py:213
  98.7 72.6 %collective-permute-done.1 = bf16[4,224,2048]{2,1,0:T(8,128)(2,1)} collective-permute-done((bf16[4,224,2048]{2,1,0:T(8,128)(2,1)}, bf16[4,224,2048]{2,1,0:T(8,128)(2,1)}, u32[]{:S(2)}, u32[]{:S(2)}) %collective-permute-start.1) | collective-permute-done | bytes 3670048 | tf_op jit(solution)/shard_map/ppermute | solution.py:59
  197.0 57.0 %collective-permute-done.5 = bf16[4,224,2048]{2,1,0:T(8,128)(2,1)} collective-permute-done((bf16[4,224,2048]{2,1,0:T(8,128)(2,1)}, bf16[4,224,2048]{2,1,0:T(8,128)(2,1)}, u32[]{:S(2)}, u32[]{:S(2)}) %collective-permute-start.5) | collective-permute-done | bytes 3670048 | tf_op jit(solution)/shard_map/ppermute | solution.py:59
  266.2 7.0 fusion.308
  273.2 15.4 %fusion.314 = bf16[6,32,4,8,128]{4,3,2,1,0:T(8,128)(2,1)S(1)} fusion(bf16[6,256,2048]{2,1,0:T(8,128)(2,1)S(1)} %copy-done.86, bf16[2,2048,512]{2,1,0:T(8,128)(2,1)S(1)} %copy-done.92), kind=kOutput, calls=%fused_computation.299 | convolution fusion | flops 3222011904 | bytes 9961472 | tf_op jit(solution)/shard_map/btd,dk->btk/dot_general | solution.py:40
  304.5 17.1 %all-gather.9.cloned.1.call-done = bf16[6,256,2048]{2,1,0:T(8,128)(2,1)} async-done(((bf16[6,64,2048]{2,1,0:T(8,128)(2,1)}), bf16[6,256,2048]{2,1,0:T(8,128)(2,1)}) %all-gather.9.cloned.1.call-update) | async-done | bytes 6291472 | tf_op jit(solution)/shard_map/all_gather | solution.py:177
  350.4 7.9 all-to-all-start
  393.2 31.8 %all-to-all-done = bf16[4,12,64,512]{3,2,1,0:T(8,128)(2,1)} async-done(((bf16[4,12,64,512]{3,2,1,0:T(8,128)(2,1)}), bf16[4,12,64,512]{3,2,1,0:T(8,128)(2,1)}, u32[]{:S(2)}, u32[]{:S(2)}) %all-to-all-start) | async-done | bytes 3145760 | tf_op jit(solution)/shard_map/all_to_all | solution.py:194
  425.0 7.9 fusion.68
  438.1 8.8 fusion.72
  450.3 7.5 fusion.76
  464.1 8.6 fusion.80
  480.7 84.3 %all-gather.13.cloned.1.call-done = bf16[6,256,2048]{2,1,0:T(8,128)(2,1)} async-done(((bf16[6,64,2048]{2,1,0:T(8,128)(2,1)}), bf16[6,256,2048]{2,1,0:T(8,128)(2,1)}) %all-gather.13.cloned.1.call-update) | async-done | bytes 6291472 | tf_op jit(solution)/shard_map/all_gather | solution.py:177
  594.2 7.2 all-to-all-start.1
  618.3 95.3 %all-gather.11.cloned.1.call-done = bf16[6,256,2048]{2,1,0:T(8,128)(2,1)} async-done(((bf16[6,64,2048]{2,1,0:T(8,128)(2,1)}), bf16[6,256,2048]{2,1,0:T(8,128)(2,1)}) %all-gather.11.cloned.1.call-update) | async-done | bytes 6291472 | tf_op jit(solution)/shard_map/all_gather | solution.py:177
  713.6 7.5 fusion.299
  740.3 8.2 all-to-all-start.2
  769.3 12.1 all-to-all-done.2
  781.4 7.7 fusion.83
  796.4 7.5 convolution_convert_fusion
  803.9 9.2 all-to-all-start.5
  813.1 9.1 convolution_convert_fusion.1
  822.3 128.4 %all-to-all-done.5 = bf16[16,96,2048]{2,1,0:T(8,128)(2,1)} async-done(((bf16[16,96,2048]{2,1,0:T(8,128)(2,1)}), bf16[16,96,2048]{2,1,0:T(8,128)(2,1)}, u32[]{:S(2)}, u32[]{:S(2)}) %all-to-all-start.5) | async-done | bytes 6291488 | tf_op jit(solution)/shard_map/all_to_all | solution.py:121
  955.8 13.0 fusion.129
  968.8 13.0 fusion.132
  988.6 104.4 %all-to-all-done.3 = bf16[16,96,2048]{2,1,0:T(8,128)(2,1)} async-done(((bf16[16,96,2048]{2,1,0:T(8,128)(2,1)}), bf16[16,96,2048]{2,1,0:T(8,128)(2,1)}, u32[]{:S(2)}, u32[]{:S(2)}) %all-to-all-start.3) | async-done | bytes 6291488 | tf_op jit(solution)/shard_map/all_to_all | solution.py:121
  1097.8 13.0 fusion.135
  1110.8 13.0 fusion.138
  1130.6 104.9 %all-to-all-done.6 = bf16[16,96,2048]{2,1,0:T(8,128)(2,1)} async-done(((bf16[16,96,2048]{2,1,0:T(8,128)(2,1)}), bf16[16,96,2048]{2,1,0:T(8,128)(2,1)}, u32[]{:S(2)}, u32[]{:S(2)}) %all-to-all-start.6) | async-done | bytes 6291488 | tf_op jit(solution)/shard_map/all_to_all | solution.py:130
  1258.0 16.3 %multiply_reduce_fusion.1 = f32[768,2048]{1,0:T(8,128)} fusion(f32[768,2]{0,1:T(2,128)S(1)} %broadcast_divide_fusion, bf16[1536,2048,1]{1,0,2:T(8,128)(2,1)} %bitcast.145, s32[1536]{0:T(1024)S(1)} %eq.179, s32[768,2]{0,1:T(2,128)S(1)} %copy-done.79), kind=kOutput, calls=%fused_computation.5 | convolution fusion | flops 9670754304 | bytes 12601344 | tf_op jit(solution)/shard_map/ncs,sd->ncd/dot_general | solution.py:138
  1274.3 103.7 %all-to-all-done.4 = bf16[16,96,2048]{2,1,0:T(8,128)(2,1)} async-done(((bf16[16,96,2048]{2,1,0:T(8,128)(2,1)}), bf16[16,96,2048]{2,1,0:T(8,128)(2,1)}, u32[]{:S(2)}, u32[]{:S(2)}) %all-to-all-start.4) | async-done | bytes 6291488 | tf_op jit(solution)/shard_map/all_to_all | solution.py:130
  1378.0 16.6 %multiply_reduce_fusion = f32[768,2048]{1,0:T(8,128)} fusion(f32[768,2]{0,1:T(2,128)S(1)} %broadcast_divide_fusion, bf16[1536,2048]{1,0:T(8,128)(2,1)} %bitcast.128, s32[1536]{0:T(1024)S(1)} %eq.169, s32[768,2]{0,1:T(2,128)S(1)} %copy-done.79), kind=kOutput, calls=%fused_computation.4 | convolution fusion | flops 9670754304 | bytes 12601344 | tf_op jit(solution)/shard_map/ncs,sd->ncd/dot_general | solution.py:138
  (385 shorter events, 313.3 us)
Async XLA Ops:
  7.2 1247.6 %copy-start = (f32[2048,64]{0,1:T(8,128)S(1)}, f32[2048,64]{0,1:T(8,128)}, u32[]{:S(2)}) copy-start(f32[2048,64]{0,1:T(8,128)} %param.26) | copy-start | bytes 1572868
  7.2 83.7 %all-gather.15.cloned.1.call-start = ((), (), s32[]{:S(2)}) async-start(), calls=%async_computation.11 | async-start | bytes 4587520 | tf_op jit(solution)/shard_map/all_gather | solution.py:213
  21.1 245.1 %all-gather.7.cloned.1.call-start = ((), (), s32[]{:S(2)}) async-start(), calls=%async_computation.7 | async-start | bytes 7864320 | tf_op jit(solution)/shard_map/all_gather | solution.py:177
  90.9 230.7 %all-gather.9.cloned.1.call-start = ((), (), s32[]{:S(2)}) async-start(), calls=%async_computation.8 | async-start | bytes 7864320 | tf_op jit(solution)/shard_map/all_gather | solution.py:177
  91.4 79.9 %collective-permute-start.1 = (bf16[4,224,2048]{2,1,0:T(8,128)(2,1)}, bf16[4,224,2048]{2,1,0:T(8,128)(2,1)}, u32[]{:S(2)}, u32[]{:S(2)}) collective-permute-start(bf16[4,224,2048]{2,1,0:T(8,128)(2,1)} %bitcast.663), channel_id=1, source_target_pairs={{0,2},{1,3},{2,0},{3,1},{4,6},{5,7},{6,4},{7,5},{8,10},{9,11},{10,... | collective-permute-start | bytes 11010056 | tf_op jit(solution)/shard_map/ppermute | solution.py:59
  91.8 81.5 %collective-permute-start.3 = (bf16[4,224,2048]{2,1,0:T(8,128)(2,1)}, bf16[4,224,2048]{2,1,0:T(8,128)(2,1)}, u32[]{:S(2)}, u32[]{:S(2)}) collective-permute-start(bf16[4,224,2048]{2,1,0:T(8,128)(2,1)} %bitcast.664), channel_id=1, source_target_pairs={{0,16},{16,0},{1,17},{17,1},{2,18},{18,2},{3,19},{19,3},{4,20},{20... | collective-permute-start | bytes 11010056 | tf_op jit(solution)/shard_map/ppermute | solution.py:59
  94.2 91.4 %collective-permute-start = (bf16[4,224,2048]{2,1,0:T(8,128)(2,1)}, bf16[4,224,2048]{2,1,0:T(8,128)(2,1)}, u32[]{:S(2)}, u32[]{:S(2)}) collective-permute-start(bf16[4,224,2048]{2,1,0:T(8,128)(2,1)} %bitcast.665), channel_id=1, source_target_pairs={{0,1},{1,0},{2,3},{3,2},{4,5},{5,4},{6,7},{7,6},{8,9},{9,8},{10,11... | collective-permute-start | bytes 11010056 | tf_op jit(solution)/shard_map/ppermute | solution.py:59
  97.1 85.2 %copy-start.32 = (pred[256,256]{0,1:T(8,128)(4,1)}, pred[256,256]{0,1:T(8,128)(4,1)S(1)}, u32[]{:S(2)}) copy-start(pred[256,256]{0,1:T(8,128)(4,1)S(1)} %get-tuple-element.173) | copy-start | bytes 196612
  97.1 85.2 %copy-start.34 = (pred[256,256]{0,1:T(8,128)(4,1)}, pred[256,256]{0,1:T(8,128)(4,1)S(1)}, u32[]{:S(2)}) copy-start(pred[256,256]{0,1:T(8,128)(4,1)S(1)} %get-tuple-element.174) | copy-start | bytes 196612
  97.2 85.1 %copy-start.36 = (pred[256,256]{0,1:T(8,128)(4,1)}, pred[256,256]{0,1:T(8,128)(4,1)S(1)}, u32[]{:S(2)}) copy-start(pred[256,256]{0,1:T(8,128)(4,1)S(1)} %get-tuple-element.175) | copy-start | bytes 196612
  97.2 85.1 %copy-start.38 = (pred[256,256]{0,1:T(8,128)(4,1)}, pred[256,256]{0,1:T(8,128)(4,1)S(1)}, u32[]{:S(2)}) copy-start(pred[256,256]{0,1:T(8,128)(4,1)S(1)} %get-tuple-element.176) | copy-start | bytes 196612
  97.3 85.0 %copy-start.40 = (pred[256,256]{0,1:T(8,128)(4,1)}, pred[256,256]{0,1:T(8,128)(4,1)S(1)}, u32[]{:S(2)}) copy-start(pred[256,256]{0,1:T(8,128)(4,1)S(1)} %get-tuple-element.177) | copy-start | bytes 196612
  97.3 85.0 %copy-start.42 = (pred[256,256]{0,1:T(8,128)(4,1)}, pred[256,256]{0,1:T(8,128)(4,1)S(1)}, u32[]{:S(2)}) copy-start(pred[256,256]{0,1:T(8,128)(4,1)S(1)} %get-tuple-element.178) | copy-start | bytes 196612
  97.3 85.0 %copy-start.44 = (pred[256,256]{0,1:T(8,128)(4,1)}, pred[256,256]{0,1:T(8,128)(4,1)S(1)}, u32[]{:S(2)}) copy-start(pred[256,256]{0,1:T(8,128)(4,1)S(1)} %get-tuple-element.179) | copy-start | bytes 196612
  97.3 85.0 %copy-start.46 = (pred[256,256]{0,1:T(8,128)(4,1)}, pred[256,256]{0,1:T(8,128)(4,1)S(1)}, u32[]{:S(2)}) copy-start(pred[256,256]{0,1:T(8,128)(4,1)S(1)} %get-tuple-element.180) | copy-start | bytes 196612
  97.4 84.9 %copy-start.48 = (pred[256,256]{0,1:T(8,128)(4,1)}, pred[256,256]{0,1:T(8,128)(4,1)S(1)}, u32[]{:S(2)}) copy-start(pred[256,256]{0,1:T(8,128)(4,1)S(1)} %get-tuple-element.181) | copy-start | bytes 196612
  97.4 84.9 %copy-start.50 = (pred[256,256]{0,1:T(8,128)(4,1)}, pred[256,256]{0,1:T(8,128)(4,1)S(1)}, u32[]{:S(2)}) copy-start(pred[256,256]{0,1:T(8,128)(4,1)S(1)} %get-tuple-element.182) | copy-start | bytes 196612
  171.3 83.7 %collective-permute-start.2 = (bf16[4,224,2048]{2,1,0:T(8,128)(2,1)}, bf16[4,224,2048]{2,1,0:T(8,128)(2,1)}, u32[]{:S(2)}, u32[]{:S(2)}) collective-permute-start(bf16[4,224,2048]{2,1,0:T(8,128)(2,1)} %collective-permute-done.1), channel_id=1, source_target_pairs={{0,1},{1,0},{2,3},{3,2},{4,5},{5,4},{6,7},{7,6},{8,9},{9,8},{10,11... | collective-permute-start | bytes 11010056 | tf_op jit(solution)/shard_map/ppermute | solution.py:59
  173.2 80.7 %collective-permute-start.5 = (bf16[4,224,2048]{2,1,0:T(8,128)(2,1)}, bf16[4,224,2048]{2,1,0:T(8,128)(2,1)}, u32[]{:S(2)}, u32[]{:S(2)}) collective-permute-start(bf16[4,224,2048]{2,1,0:T(8,128)(2,1)} %collective-permute-done.3), channel_id=1, source_target_pairs={{0,2},{1,3},{2,0},{3,1},{4,6},{5,7},{6,4},{7,5},{8,10},{9,11},{10,... | collective-permute-start | bytes 11010056 | tf_op jit(solution)/shard_map/ppermute | solution.py:59
  178.2 81.9 %collective-permute-start.4 = (bf16[4,224,2048]{2,1,0:T(8,128)(2,1)}, bf16[4,224,2048]{2,1,0:T(8,128)(2,1)S(1)}, u32[]{:S(2)}, u32[]{:S(2)}) collective-permute-start(bf16[4,224,2048]{2,1,0:T(8,128)(2,1)} %collective-permute-done.3), channel_id=1, source_target_pairs={{0,1},{1,0},{2,3},{3,2},{4,5},{5,4},{6,7},{7,6},{8,9},{9,8},{10,11... | collective-permute-start | bytes 11010056 | tf_op jit(solution)/shard_map/ppermute | solution.py:59
  254.0 115.2 %collective-permute-start.6 = (bf16[4,224,2048]{2,1,0:T(8,128)(2,1)}, bf16[4,224,2048]{2,1,0:T(8,128)(2,1)}, u32[]{:S(2)}, u32[]{:S(2)}) collective-permute-start(bf16[4,224,2048]{2,1,0:T(8,128)(2,1)} %collective-permute-done.5), channel_id=1, source_target_pairs={{0,1},{1,0},{2,3},{3,2},{4,5},{5,4},{6,7},{7,6},{8,9},{9,8},{10,11... | collective-permute-start | bytes 11010056 | tf_op jit(solution)/shard_map/ppermute | solution.py:59
  350.4 74.6 %all-to-all-start = ((bf16[4,12,64,512]{3,2,1,0:T(8,128)(2,1)}), bf16[4,12,64,512]{3,2,1,0:T(8,128)(2,1)}, u32[]{:S(2)}, u32[]{:S(2)}) async-start(bf16[4,12,64,512]{3,2,1,0:T(8,128)(2,1)} %copy.151), calls=%async_computation | async-start | bytes 6291456 | tf_op jit(solution)/shard_map/all_to_all | solution.py:194
  358.3 206.7 %all-gather.13.cloned.1.call-start = ((), (), s32[]{:S(2)}) async-start(), calls=%async_computation.10 | async-start | bytes 7864320 | tf_op jit(solution)/shard_map/all_gather | solution.py:177
  450.1 263.5 %all-gather.11.cloned.1.call-start = ((), (), s32[]{:S(2)}) async-start(), calls=%async_computation.9 | async-start | bytes 7864320 | tf_op jit(solution)/shard_map/all_gather | solution.py:177
  594.2 119.4 %all-to-all-start.1 = ((bf16[4,6,64,512]{3,2,1,0:T(8,128)(2,1)}), bf16[4,6,64,512]{3,2,1,0:T(8,128)(2,1)S(1)}, u32[]{:S(2)}, u32[]{:S(2)}) async-start(bf16[4,6,64,512]{3,2,1,0:T(8,128)(2,1)} %copy.159), calls=%async_computation.1 | async-start | bytes 3145728 | tf_op jit(solution)/shard_map/all_to_all | solution.py:194
  601.5 119.6 %copy-start.74 = (s32[768,2]{0,1:T(2,128)}, s32[768,2]{0,1:T(2,128)S(1)}, u32[]{:S(2)}) copy-start(s32[768,2]{0,1:T(2,128)S(1)} %reshape.825) | copy-start | bytes 18436
  613.0 108.0 %copy-start.78 = (s32[768,2]{0,1:T(2,128)}, s32[768,2]{0,1:T(2,128)S(1)}, u32[]{:S(2)}) copy-start(s32[768,2]{0,1:T(2,128)S(1)} %compare_select_fusion) | copy-start | bytes 18436
  740.3 41.1 %all-to-all-start.2 = ((bf16[4,6,64,512]{3,2,1,0:T(8,128)(2,1)}), bf16[4,6,64,512]{3,2,1,0:T(8,128)(2,1)}, u32[]{:S(2)}, u32[]{:S(2)}) async-start(bf16[4,6,64,512]{3,2,1,0:T(8,128)(2,1)} %copy.165), calls=%async_computation.2 | async-start | bytes 3145728 | tf_op jit(solution)/shard_map/all_to_all | solution.py:194
  803.9 146.8 %all-to-all-start.5 = ((bf16[16,96,2048]{2,1,0:T(8,128)(2,1)}), bf16[16,96,2048]{2,1,0:T(8,128)(2,1)}, u32[]{:S(2)}, u32[]{:S(2)}) async-start(bf16[16,96,2048]{2,1,0:T(8,128)(2,1)} %bitcast.650), calls=%async_computation.5 | async-start | bytes 12582912 | tf_op jit(solution)/shard_map/all_to_all | solution.py:121
  950.7 142.3 %all-to-all-start.3 = ((bf16[16,96,2048]{2,1,0:T(8,128)(2,1)}), bf16[16,96,2048]{2,1,0:T(8,128)(2,1)}, u32[]{:S(2)}, u32[]{:S(2)}) async-start(bf16[16,96,2048]{2,1,0:T(8,128)(2,1)} %bitcast.649), calls=%async_computation.3 | async-start | bytes 12582912 | tf_op jit(solution)/shard_map/all_to_all | solution.py:121
  1093.0 142.4 %all-to-all-start.6 = ((bf16[16,96,2048]{2,1,0:T(8,128)(2,1)}), bf16[16,96,2048]{2,1,0:T(8,128)(2,1)}, u32[]{:S(2)}, u32[]{:S(2)}) async-start(bf16[16,96,2048]{2,1,0:T(8,128)(2,1)} %bitcast.647), calls=%async_computation.6 | async-start | bytes 12582912 | tf_op jit(solution)/shard_map/all_to_all | solution.py:130
  1235.5 142.6 %all-to-all-start.4 = ((bf16[16,96,2048]{2,1,0:T(8,128)(2,1)}), bf16[16,96,2048]{2,1,0:T(8,128)(2,1)}, u32[]{:S(2)}, u32[]{:S(2)}) async-start(bf16[16,96,2048]{2,1,0:T(8,128)(2,1)} %bitcast.646), calls=%async_computation.4 | async-start | bytes 12582912 | tf_op jit(solution)/shard_map/all_to_all | solution.py:130
  (85 other events, 1785.0 us)
Sparse Core Ops, SparseCore 0:
  21.2 69.6 all-gather.14
  92.5 113.5 all-gather.6
  208.2 113.3 all-gather.8
  450.2 114.7 all-gather.12
  566.9 146.5 all-gather.10
